TPU v7x, 32 devices: a whole 2x2x4 slice. The times are simulated.
32 devices in a mesh: grp: 2 (over y), lat: 4 (over z), lay: 4 (over x, core).
Axes of the slice: x: 2, y: 2, z: 4, core: 2. Of those that a mesh axis runs over, the one named last changes fastest.
Arguments:
- acts: bfloat16 [128, 4, 1280], P(('grp', 'lat'), 'lay'), parts along dimension 0, may hold values from -6 to 6
- w_enc: bfloat16 [4, 1280, 1536], P('lay', None, 'lat'), may hold values from -0.078125 to 0.078125
- w_dec: bfloat16 [1536, 4, 1280], P('lat', 'lay'), may hold values from -0.15625 to 0.15625
- b_enc: float32 [1536], P('lat'), may hold values from -3 to 3
- b_dec: float32 [4, 1280], P('lay'), may hold values from -3 to 3
Outputs:
- lat_grad: bfloat16 [128, 1536], P('grp', 'lat'), parts along dimension 0
- enc_grad: bfloat16 [8, 1280, 1536], P(('grp', 'lay'), None, 'lat'), parts along dimension 0
- dec_grad: bfloat16 [1536, 8, 1280], P('lat', ('grp', 'lay')), parts along dimension 1
There are 2 independent parts, one for each index of `grp`. A program takes and returns all parts, laid end to end along the dimension named above; an argument that names none is the same for every part. Nothing has to cross between parts.
All inputs are finite; a program needn't handle non-finite values.
Results may differ from a plain program's by a relative error of at most 0.023.
Values may be sent and summed in bfloat16 or wider, within the bound.
A program may use at most 64 MiB of HBM per device.

v0:
```python
import functools

import jax
import jax.numpy as jnp
from jax import lax
from jax.experimental import pallas as pl
from jax.experimental.pallas import tpu as pltpu
from jax.sharding import PartitionSpec as P

MESH = pl.DeviceIdType.MESH
F32, BF16 = jnp.float32, jnp.bfloat16


def flip(v, j):
    out, bit = v, 1
    while bit <= j:
        if j & bit:
            out = out + bit * (1 - 2 * lax.rem(lax.div(v, bit), 2))
        bit *= 2
    return out


def step(
    n_lat, n_lay, groups, acts_hbm, wenc_hbm, wdec_hbm, benc_ref, bdec_ref,
    lat_out, acts_t, dec_out,
    acts_all, wenc, wdec, wdec_t, pre_buf, back_buf, rec_mine, rec_buf, err_all, code_all, slope,
    load, acts_s, acts_r, pre_s, pre_r, rec_s, rec_r, err_s, err_r, back_s, back_r,
):
    z, l = lax.axis_index("lat"), lax.axis_index("lay")
    row_dev, wide = acts_all.shape[1:]
    rows, lat_dev = n_lat * row_dev, wenc.shape[1]
    size = n_lat // groups
    part = size * row_dev

    load_acts = pltpu.make_async_copy(acts_hbm, acts_all.at[z], load.at[0])
    load_enc = pltpu.make_async_copy(wenc_hbm, wenc, load.at[1])
    load_dec = pltpu.make_async_copy(wdec_hbm, wdec, load.at[2])
    load_acts.start()
    load_enc.start()
    load_dec.start()

    if groups > 1:
        dest = source = lambda j: flip(z, j)
    else:
        dest = lambda j: lax.rem(z + j, n_lat)
        source = lambda j: lax.rem(z + n_lat - j, n_lat)
    group = [flip(lax.div(z, size), g) if groups > 1 else 0 for g in range(groups)]

    def lay_peer(k):
        return {"lay": lax.rem(l + k, n_lay)}

    barrier = pltpu.get_barrier_semaphore()
    for j in reversed(range(1, n_lat)):
        pl.semaphore_signal(
            barrier, inc=1, device_id={"lat": dest(j)}, device_id_type=MESH
        )
    for k in range(1, n_lay):
        pl.semaphore_signal(barrier, inc=1, device_id=lay_peer(k), device_id_type=MESH)
    pl.semaphore_wait(barrier, n_lat + n_lay - 2)

    started = []

    def send(src, dst, send_sem, recv_sem, peer):
        copy = pltpu.make_async_remote_copy(
            src_ref=src, dst_ref=dst, send_sem=send_sem, recv_sem=recv_sem,
            device_id=peer, device_id_type=MESH,
        )
        copy.start()
        started.append(copy)
        return copy

    def to_lat(buf, sent, received):
        return {
            j: send(buf.at[z], buf.at[z], sent.at[j], received.at[j], {"lat": dest(j)})
            for j in range(1, n_lat)
        }

    def to_lay(buf, g, sent, received):
        block = buf.at[l, group[g]]
        return [
            send(block, block, sent.at[g, k], received.at[g, k], lay_peer(k))
            for k in range(1, n_lay)
        ]

    def arrive(copies, g):
        for j in range(g * size, (g + 1) * size):
            if j:
                copies[j].wait_recv()

    def rows_of(buf, g):
        return buf[pl.ds(group[g] * size, size)].reshape(part, wide)

    def total(buf, g):
        whole = buf[0, group[g]].astype(F32)
        for i in range(1, n_lay):
            whole += buf[i, group[g]].astype(F32)
        return whole

    load_acts.wait()
    acts_copies = to_lat(acts_all, acts_s, acts_r)
    load_enc.wait()
    pre_copies, rec_copies = {}, {}

    def encode(g):
        arrive(acts_copies, g)
        pre = jnp.dot(rows_of(acts_all, g), wenc[...], preferred_element_type=F32)
        pre_buf[l, group[g]] = pre.astype(BF16)
        pre_copies[g] = to_lay(pre_buf, g, pre_s, pre_r)

    def decode(g):
        for copy in pre_copies[g]:
            copy.wait_recv()
        x = 4.0 * (total(pre_buf, g) + benc_ref[...].reshape(1, lat_dev))
        e = jnp.exp(-jnp.abs(x))
        code = (0.25 * (jnp.maximum(x, 0.0) + jnp.log1p(e))).astype(BF16)
        rec = jnp.dot(code, wdec[...], preferred_element_type=F32).astype(BF16)
        rec_mine[pl.ds(group[g] * size, size)] = rec.reshape(size, row_dev, wide)
        for j in range(g * size, (g + 1) * size):
            if j:
                rec_copies[j] = send(
                    rec_mine.at[dest(j)], rec_buf.at[z], rec_s.at[j], rec_r.at[j],
                    {"lat": dest(j)},
                )
        code_all[group[g]] = code
        slope[group[g]] = jnp.where(x >= 0.0, 1.0, e) / (1.0 + e)

    for g in range(groups):
        encode(g)
        if g == 0:
            load_dec.wait()
    for g in [*range(1, groups), 0]:
        decode(g)
    wdec_t[...] = wdec[...].astype(F32).T.astype(BF16)
    acts_t[...] = acts_all[...].reshape(rows, wide).astype(F32).T.astype(BF16)
    code_t = code_all[...].reshape(rows, lat_dev).astype(F32).T.astype(BF16)
    err = bdec_ref[...] - acts_all[z].astype(F32) + rec_mine[z].astype(F32)
    for j in range(1, n_lat):
        rec_copies[j].wait_recv()
        err += rec_buf[source(j)].astype(F32)
    err_all[z] = err.astype(BF16)
    err_copies = to_lat(err_all, err_s, err_r)
    back_copies = {}
    for g in range(groups):
        arrive(err_copies, g)
        back = jnp.dot(rows_of(err_all, g), wdec_t[...], preferred_element_type=F32)
        back_buf[l, group[g]] = back.astype(BF16)
        back_copies[g] = to_lay(back_buf, g, back_s, back_r)
    errs = err_all[...].reshape(rows, wide)
    dec_out[...] = jnp.dot(code_t, errs, preferred_element_type=F32).astype(BF16)
    for g in range(groups):
        for copy in back_copies[g]:
            copy.wait_recv()
        lat_out[group[g]] = (total(back_buf, g) * slope[group[g]]).astype(BF16)
    for copy in started:
        copy.wait_send()


def finish(chunks, lat, acts_t, dec, lat_hbm, enc_hbm, dec_hbm, enc, sems):
    rows, lat_dev = lat.shape[0] * lat.shape[1], lat.shape[2]
    copies = [
        pltpu.make_async_copy(dec, dec_hbm, sems.at[0]),
        pltpu.make_async_copy(lat, lat_hbm, sems.at[1]),
    ]
    for copy in copies:
        copy.start()
    grad = lat[...].reshape(rows, lat_dev)
    tall = enc.shape[0] // chunks
    for c in range(chunks):
        cut = pl.ds(c * tall, tall)
        enc[cut] = jnp.dot(acts_t[cut], grad, preferred_element_type=F32).astype(BF16)
        copy = pltpu.make_async_copy(enc.at[cut], enc_hbm.at[cut], sems.at[2 + c])
        copy.start()
        copies.append(copy)
    for copy in copies:
        copy.wait()


def solution(mesh):
    n_lat, n_lay = mesh.shape["lat"], mesh.shape["lay"]

    def on_device(acts, w_enc, w_dec, b_enc, b_dec):
        row_dev, lay_dev, width = acts.shape
        lat_dev = w_enc.shape[2]
        wide, rows = lay_dev * width, n_lat * row_dev
        hbm = pl.BlockSpec(memory_space=pltpu.HBM)
        vmem = pl.BlockSpec(memory_space=pltpu.VMEM)
        dma = pltpu.SemaphoreType.DMA
        groups = 4 if n_lat & (n_lat - 1) == 0 and n_lat % 4 == 0 else 1
        part = rows // groups
        chunks = 5 if wide % 80 == 0 else 1
        lat_part, acts_t, dec_part = pl.pallas_call(
            functools.partial(step, n_lat, n_lay, groups),
            out_shape=[
                pltpu.VMEM((groups, part, lat_dev), BF16),
                pltpu.VMEM((wide, rows), BF16),
                pltpu.VMEM((lat_dev, wide), BF16),
            ],
            in_specs=[hbm, hbm, hbm, vmem, vmem],
            out_specs=[vmem, vmem, vmem],
            scratch_shapes=[
                pltpu.VMEM((n_lat, row_dev, wide), BF16),
                pltpu.VMEM((wide, lat_dev), BF16),
                pltpu.VMEM((lat_dev, wide), BF16),
                pltpu.VMEM((wide, lat_dev), BF16),
                pltpu.VMEM((n_lay, groups, part, lat_dev), BF16),
                pltpu.VMEM((n_lay, groups, part, lat_dev), BF16),
                pltpu.VMEM((n_lat, row_dev, wide), BF16),
                pltpu.VMEM((n_lat, row_dev, wide), BF16),
                pltpu.VMEM((n_lat, row_dev, wide), BF16),
                pltpu.VMEM((groups, part, lat_dev), BF16),
                pltpu.VMEM((groups, part, lat_dev), F32),
                dma((3,)),
                dma((n_lat,)), dma((n_lat,)),
                dma((groups, n_lay)), dma((groups, n_lay)),
                dma((n_lat,)), dma((n_lat,)),
                dma((n_lat,)), dma((n_lat,)),
                dma((groups, n_lay)), dma((groups, n_lay)),
            ],
            compiler_params=pltpu.CompilerParams(collective_id=0, has_side_effects=True),
            cost_estimate=pl.CostEstimate(
                flops=8 * rows * wide * lat_dev,
                bytes_accessed=4 * wide * lat_dev,
                transcendentals=0,
            ),
        )(
            acts.reshape(row_dev, wide),
            w_enc.reshape(wide, lat_dev),
            w_dec.reshape(lat_dev, wide),
            b_enc,
            b_dec.reshape(1, wide),
        )
        lat_grad, enc_grad, dec_grad = pl.pallas_call(
            functools.partial(finish, chunks),
            out_shape=[
                jax.ShapeDtypeStruct((groups, part, lat_dev), BF16),
                jax.ShapeDtypeStruct((wide, lat_dev), BF16),
                jax.ShapeDtypeStruct((lat_dev, wide), BF16),
            ],
            in_specs=[vmem, vmem, vmem],
            out_specs=[hbm, hbm, hbm],
            scratch_shapes=[pltpu.VMEM((wide, lat_dev), BF16), dma((2 + chunks,))],
            compiler_params=pltpu.CompilerParams(vmem_limit_bytes=8 * wide * lat_dev),
            cost_estimate=pl.CostEstimate(
                flops=2 * rows * wide * lat_dev,
                bytes_accessed=4 * wide * lat_dev,
                transcendentals=0,
            ),
        )(lat_part, acts_t, dec_part)
        return (
            lat_grad.reshape(rows, lat_dev),
            enc_grad.reshape(lay_dev, width, lat_dev),
            dec_grad.reshape(lat_dev, lay_dev, width),
        )

    in_specs = (
        P(("grp", "lat"), "lay", None),
        P("lay", None, "lat"),
        P("lat", "lay", None),
        P("lat"),
        P("lay", None),
    )
    out_specs = (P("grp", "lat"), P(("grp", "lay"), None, "lat"), P("lat", ("grp", "lay"), None))
    return jax.shard_map(
        on_device, mesh=mesh, in_specs=in_specs, out_specs=out_specs, check_vma=False
    )
```

profile of v0, /device:TPU:0, one launch (start us, length us, event | category | flops | bytes accessed | tf_op | source)
XLA Modules:
  0.0 29.1 jit_solution(7670284543554389979)
XLA Ops:
  0.6 27.2 %shard_map.76 = (bf16[4,16,384]{2,1,0:T(8,128)(2,1)S(1)}, bf16[1280,64]{1,0:T(8,128)(2,1)S(1)}, bf16[384,1280]{1,0:T(8,128)(2,1)S(1)}) custom-call(bf16[16,1280]{1,0:T(8,128)(2,1)} %bitcast.8, bf16[1280,384]{1,0:T(8,128)(2,1)} %bitcast.6, bf16[384,1280]{1,0:T(8,128)(2,1)} %bitcast.7, f32[384]{0:T(512)} %benc_ref.1, f32[1,1280]{1,0:T(1,128)} %bdec_ref.1), custom_call_target="tpu_custom_call" | custom-call | flops 251658240 | bytes 1966080 | tf_op jit(solution)/shard_map/pallas_call | solution.py:191
  27.8 1.3 %shard_map.77 = (bf16[4,16,384]{2,1,0:T(8,128)(2,1)}, bf16[1280,384]{1,0:T(8,128)(2,1)}, bf16[384,1280]{1,0:T(8,128)(2,1)}) custom-call(bf16[4,16,384]{2,1,0:T(8,128)(2,1)S(1)} %get-tuple-element.9.lat, bf16[1280,64]{1,0:T(8,128)(2,1)S(1)} %get-tuple-element.10.acts_t, bf16[384,1280]{1,0:T(8,128)(2,1)S(1)} %get-tuple-element.11.dec), custom_call_target="tpu_custom_call" | custom-call | flops 62914560 | bytes 1966080 | tf_op jit(solution)/shard_map/pallas_call | solution.py:232
where the time goes:
time: 29.3 us; the launch traced here: 29.1 us
  Pallas kernels  28.5 us (97%)
  between operations  0.64 us (2%)
    pallas_call x1, Pallas kernels, on_device(): pl.pallas_call(functools.partial(step, n_lat, n_lay, groups), out_shape=[...  27.2 us
    pallas_call x1, Pallas kernels, on_device(): pl.pallas_call(functools.partial(finish, chunks), out_shape=[jax.ShapeDty...  1.34 us

commit v1 on v0

--- a/solution.py
+++ b/solution.py
@@ -155,6 +155,168 @@
         copy.wait_send()
 
 
+def same(v, c):
+    return lax.div(1, 1 + (v - c) * (v - c))
+
+
+def line_step(
+    n_lat, n_lay, acts_hbm, wenc_hbm, wdec_hbm, benc_hbm, bdec_hbm,
+    lat_out, acts_t, dec_out,
+    acts_all, wenc, wdec, wdec_t, benc, bdec, pre_buf, back_buf, rec_mine, rec_buf, err_all,
+    code_all, slope,
+    load, acts_s, acts_r, pre_s, pre_r, rec_s, rec_r, err_s, err_r, back_s, back_r,
+):
+    z, l = lax.axis_index("lat"), lax.axis_index("lay")
+    row_dev, wide = acts_all.shape[1:]
+    rows, lat_dev = n_lat * row_dev, wenc.shape[1]
+    half = n_lat // 2
+    high, low = half, half - 1
+    upper = lax.div(z, half)
+    place = z + upper * (n_lat - 1 - 2 * z)
+
+    def farthest(k):
+        v = n_lat - 1 - k
+        v = v - (1 - lax.div(1, 1 + lax.div(place, v)))
+        return v + upper * (n_lat - 1 - 2 * v)
+
+    def lay_peer(k):
+        return {"lay": flip(l, k)}
+
+    barrier = pltpu.get_barrier_semaphore()
+    for k in range(n_lat - 1):
+        pl.semaphore_signal(
+            barrier, inc=1, device_id={"lat": farthest(k)}, device_id_type=MESH
+        )
+    for k in reversed(range(1, n_lay)):
+        pl.semaphore_signal(barrier, inc=1, device_id=lay_peer(k), device_id_type=MESH)
+
+    load_acts = pltpu.make_async_copy(acts_hbm, acts_all.at[z], load.at[0])
+    load_enc = pltpu.make_async_copy(wenc_hbm, wenc, load.at[1])
+    load_dec = pltpu.make_async_copy(wdec_hbm, wdec, load.at[2])
+    load_benc = pltpu.make_async_copy(benc_hbm, benc, load.at[3])
+    load_bdec = pltpu.make_async_copy(bdec_hbm, bdec, load.at[4])
+    load_acts.start()
+    load_enc.start()
+    load_dec.start()
+    load_benc.start()
+    load_bdec.start()
+
+    pl.semaphore_wait(barrier, n_lat + n_lay - 2)
+
+    def send(src, dst, send_sem, recv_sem, peer):
+        pltpu.make_async_remote_copy(
+            src_ref=src, dst_ref=dst, send_sem=send_sem, recv_sem=recv_sem,
+            device_id=peer, device_id_type=MESH,
+        ).start()
+
+    def wait(view, sem):
+        pltpu.make_async_copy(view, view, sem).wait()
+
+    def to_lay(buf, k, sent, received):
+        for j in sorted(range(1, n_lay), key=lambda j: (j < 2, j)):
+            send(buf.at[k, 0], buf.at[k, j], sent, received.at[k], lay_peer(j))
+
+    def total(buf, k, received):
+        wait(buf.at[k, pl.ds(1, n_lay - 1)], received.at[k])
+        whole = buf[k, l].astype(F32)
+        for i in range(1, n_lay):
+            whole += buf[k, flip(l, i)].astype(F32)
+        return whole
+
+    first = [
+        z + k - (1 - lax.div(1, 1 + lax.div(z + k, n_lat))) * (z + 2 * k + 1 - n_lat)
+        for k in range(n_lat)
+    ]
+
+    load_acts.wait()
+    for k in range(n_lat - 1):
+        send(acts_all.at[z], acts_all.at[z], acts_s, acts_r.at[z], {"lat": farthest(k)})
+    load_enc.wait()
+
+    def encode(k):
+        if k:
+            wait(acts_all.at[first[k]], acts_r.at[first[k]])
+        pre = jnp.dot(acts_all[first[k]], wenc[...], preferred_element_type=F32)
+        pre_buf[k, 0] = pre.astype(BF16)
+        to_lay(pre_buf, k, pre_s, pre_r)
+
+    def decode(k):
+        b = first[k]
+        x = 4.0 * (total(pre_buf, k, pre_r) + benc[...].reshape(1, lat_dev))
+        e = jnp.exp(-jnp.abs(x))
+        code = (0.25 * (jnp.maximum(x, 0.0) + jnp.log1p(e))).astype(BF16)
+        rec = jnp.dot(code, wdec[...], preferred_element_type=F32).astype(BF16)
+        rec_mine[b] = rec
+        owner = high - lax.div(b, half)
+
+        @pl.when(owner != z)
+        def _():
+            place = lax.rem(b, half)
+            send(rec_mine.at[b], rec_buf.at[place, z], rec_s, rec_r.at[place], {"lat": owner})
+
+        code_all[b] = code
+        slope[b] = jnp.where(x >= 0.0, 1.0, e) / (1.0 + e)
+
+    encode(0)
+    load_dec.wait()
+    wdec_t[...] = wdec[...].astype(F32).T.astype(BF16)
+    for k in range(1, n_lat):
+        encode(k)
+    acts_t[...] = acts_all[...].reshape(rows, wide).astype(F32).T.astype(BF16)
+    load_benc.wait()
+    load_bdec.wait()
+    for k in range(n_lat):
+        decode(k)
+
+    @pl.when((z == low) | (z == high))
+    def _():
+        for j in range(half):
+            b = half + j - same(z, high) * (2 * j + 1)
+            place = lax.rem(b, half)
+            wait(rec_buf.at[place, pl.ds(0, n_lat - 1)], rec_r.at[place])
+            err = bdec[...] - acts_all[b].astype(F32) + rec_mine[b].astype(F32)
+            for i in range(1, n_lat):
+                err += rec_buf[place, flip(z, i)].astype(F32)
+            err_all[b] = err.astype(BF16)
+            for k in range(n_lat - 1):
+                send(err_all.at[b], err_all.at[b], err_s, err_r.at[b], {"lat": farthest(k)})
+
+    code_t = code_all[...].reshape(rows, lat_dev).astype(F32).T.astype(BF16)
+    second = []
+    for k in range(n_lat):
+        up = half + k if k < half else n_lat - 1 - k
+        down = half - 1 - k if k < half else k
+        b = up + same(z, high) * (down - up)
+        second.append(b)
+        owner = high - lax.div(b, half)
+
+        @pl.when(owner != z)
+        def _():
+            wait(err_all.at[b], err_r.at[b])
+
+        back = jnp.dot(err_all[b], wdec_t[...], preferred_element_type=F32)
+        back_buf[k, 0] = back.astype(BF16)
+        to_lay(back_buf, k, back_s, back_r)
+    errs = err_all[...].reshape(rows, wide)
+    dec_out[...] = jnp.dot(code_t, errs, preferred_element_type=F32).astype(BF16)
+    for k in range(n_lat):
+        b = second[k]
+        lat_out[b] = (total(back_buf, k, back_r) * slope[b]).astype(BF16)
+
+    wait(acts_all.at[pl.ds(0, n_lat - 1)], acts_s)
+    wait(pre_buf.at[:, pl.ds(1, n_lay - 1)], pre_s)
+    wait(back_buf.at[:, pl.ds(1, n_lay - 1)], back_s)
+
+    @pl.when((z == low) | (z == high))
+    def _():
+        wait(rec_mine.at[pl.ds(0, half)], rec_s)
+        wait(rec_buf.at[:, pl.ds(0, n_lat - 1)], err_s)
+
+    @pl.when((z != low) & (z != high))
+    def _():
+        wait(rec_mine, rec_s)
+
+
 def finish(chunks, lat, acts_t, dec, lat_hbm, enc_hbm, dec_hbm, enc, sems):
     rows, lat_dev = lat.shape[0] * lat.shape[1], lat.shape[2]
     copies = [
@@ -185,28 +347,56 @@
         hbm = pl.BlockSpec(memory_space=pltpu.HBM)
         vmem = pl.BlockSpec(memory_space=pltpu.VMEM)
         dma = pltpu.SemaphoreType.DMA
+        line = n_lat in (2, 4) and n_lay & (n_lay - 1) == 0
         groups = 4 if n_lat & (n_lat - 1) == 0 and n_lat % 4 == 0 else 1
+        if line:
+            groups = n_lat
         part = rows // groups
         chunks = 5 if wide % 80 == 0 else 1
-        lat_part, acts_t, dec_part = pl.pallas_call(
-            functools.partial(step, n_lat, n_lay, groups),
-            out_shape=[
+        out_shape = [
+            pltpu.VMEM((groups, part, lat_dev), BF16),
+            pltpu.VMEM((wide, rows), BF16),
+            pltpu.VMEM((lat_dev, wide), BF16),
+        ]
+        rows_buf = pltpu.VMEM((n_lat, row_dev, wide), BF16)
+        if line:
+            kernel = functools.partial(line_step, n_lat, n_lay)
+            in_specs = [hbm] * 5
+            lay_buf = pltpu.VMEM((groups, n_lay, part, lat_dev), BF16)
+            scratch = [
+                rows_buf,
+                pltpu.VMEM((wide, lat_dev), BF16),
+                pltpu.VMEM((lat_dev, wide), BF16),
+                pltpu.VMEM((wide, lat_dev), BF16),
+                pltpu.VMEM((lat_dev,), F32),
+                pltpu.VMEM((1, wide), F32),
+                lay_buf,
+                lay_buf,
+                rows_buf,
+                pltpu.VMEM((n_lat // 2, n_lat, row_dev, wide), BF16),
+                rows_buf,
                 pltpu.VMEM((groups, part, lat_dev), BF16),
-                pltpu.VMEM((wide, rows), BF16),
-                pltpu.VMEM((lat_dev, wide), BF16),
-            ],
-            in_specs=[hbm, hbm, hbm, vmem, vmem],
-            out_specs=[vmem, vmem, vmem],
-            scratch_shapes=[
-                pltpu.VMEM((n_lat, row_dev, wide), BF16),
+                pltpu.VMEM((groups, part, lat_dev), F32),
+                dma((5,)),
+                dma, dma((n_lat,)),
+                dma, dma((groups,)),
+                dma, dma((n_lat // 2,)),
+                dma, dma((n_lat,)),
+                dma, dma((groups,)),
+            ]
+        else:
+            kernel = functools.partial(step, n_lat, n_lay, groups)
+            in_specs = [hbm, hbm, hbm, vmem, vmem]
+            scratch = [
+                rows_buf,
                 pltpu.VMEM((wide, lat_dev), BF16),
                 pltpu.VMEM((lat_dev, wide), BF16),
                 pltpu.VMEM((wide, lat_dev), BF16),
                 pltpu.VMEM((n_lay, groups, part, lat_dev), BF16),
                 pltpu.VMEM((n_lay, groups, part, lat_dev), BF16),
-                pltpu.VMEM((n_lat, row_dev, wide), BF16),
-                pltpu.VMEM((n_lat, row_dev, wide), BF16),
-                pltpu.VMEM((n_lat, row_dev, wide), BF16),
+                rows_buf,
+                rows_buf,
+                rows_buf,
                 pltpu.VMEM((groups, part, lat_dev), BF16),
                 pltpu.VMEM((groups, part, lat_dev), F32),
                 dma((3,)),
@@ -215,7 +405,13 @@
                 dma((n_lat,)), dma((n_lat,)),
                 dma((n_lat,)), dma((n_lat,)),
                 dma((groups, n_lay)), dma((groups, n_lay)),
-            ],
+            ]
+        lat_part, acts_t, dec_part = pl.pallas_call(
+            kernel,
+            out_shape=out_shape,
+            in_specs=in_specs,
+            out_specs=[vmem, vmem, vmem],
+            scratch_shapes=scratch,
             compiler_params=pltpu.CompilerParams(collective_id=0, has_side_effects=True),
             cost_estimate=pl.CostEstimate(
                 flops=8 * rows * wide * lat_dev,

time: 29.3 us -> 26.1 us (0.89)
  Pallas kernels: 28.5 us -> 25.3 us
    pallas_call x1, Pallas kernels: 27.2 us -> 24 us  [on_device(): pl.pallas_call(kernel, out_shape=out_shape, in_specs=in_specs, out_specs=...]
where the time goes in v1:
time: 26.1 us; the launch traced here: 26 us
  Pallas kernels  25.3 us (97%)
  between operations  0.64 us (2%)
    pallas_call x1, Pallas kernels, on_device(): pl.pallas_call(kernel, out_shape=out_shape, in_specs=in_specs, out_specs=...  24 us
    pallas_call x1, Pallas kernels, on_device(): pl.pallas_call(functools.partial(finish, chunks), out_shape=[jax.ShapeDty...  1.34 us

profile of v1, /device:TPU:0, one launch (start us, length us, event | category | flops | bytes accessed | tf_op | source)
XLA Modules:
  0.0 26.0 jit_solution(8654690542172154881)
XLA Ops:
  0.6 24.0 %shard_map.76 = (bf16[4,16,384]{2,1,0:T(8,128)(2,1)S(1)}, bf16[1280,64]{1,0:T(8,128)(2,1)S(1)}, bf16[384,1280]{1,0:T(8,128)(2,1)S(1)}) custom-call(bf16[16,1280]{1,0:T(8,128)(2,1)} %bitcast.8, bf16[1280,384]{1,0:T(8,128)(2,1)} %bitcast.6, bf16[384,1280]{1,0:T(8,128)(2,1)} %bitcast.7, f32[384]{0:T(512)} %benc_hbm.1, f32[1,1280]{1,0:T(1,128)} %bdec_hbm.1), custom_call_target="tpu_custom_call" | custom-call | flops 251658240 | bytes 1966080 | tf_op jit(solution)/shard_map/pallas_call | solution.py:409
  24.6 1.3 %shard_map.77 = (bf16[4,16,384]{2,1,0:T(8,128)(2,1)}, bf16[1280,384]{1,0:T(8,128)(2,1)}, bf16[384,1280]{1,0:T(8,128)(2,1)}) custom-call(bf16[4,16,384]{2,1,0:T(8,128)(2,1)S(1)} %get-tuple-element.9.lat, bf16[1280,64]{1,0:T(8,128)(2,1)S(1)} %get-tuple-element.10.acts_t, bf16[384,1280]{1,0:T(8,128)(2,1)S(1)} %get-tuple-element.11.dec), custom_call_target="tpu_custom_call" | custom-call | flops 62914560 | bytes 1966080 | tf_op jit(solution)/shard_map/pallas_call | solution.py:428

commit v2 on v1

--- a/solution.py
+++ b/solution.py
@@ -159,6 +159,14 @@
     return lax.div(1, 1 + (v - c) * (v - c))
 
 
+OWNER = [2, 2, 1, 0]
+FIRST = [[0, 1, 2, 3], [1, 2, 3, 0], [2, 3, 1, 0], [3, 2, 1, 0]]
+SECOND = [[3, 2, 1, 0], [2, 3, 1, 0], [0, 1, 2, 3], [1, 0, 2, 3]]
+OWNED = [[3], [2], [1, 0], []]
+TARGETS = [[3, 2, 1], [3, 2, 0], [0, 1, 3], [0, 1, 2]]
+SPREAD = [[1, 2, 3], [3, 2, 0], [0, 1, 3], []]
+
+
 def line_step(
     n_lat, n_lay, acts_hbm, wenc_hbm, wdec_hbm, benc_hbm, bdec_hbm,
     lat_out, acts_t, dec_out,
@@ -169,24 +177,20 @@
     z, l = lax.axis_index("lat"), lax.axis_index("lay")
     row_dev, wide = acts_all.shape[1:]
     rows, lat_dev = n_lat * row_dev, wenc.shape[1]
-    half = n_lat // 2
-    high, low = half, half - 1
-    upper = lax.div(z, half)
-    place = z + upper * (n_lat - 1 - 2 * z)
-
-    def farthest(k):
-        v = n_lat - 1 - k
-        v = v - (1 - lax.div(1, 1 + lax.div(place, v)))
-        return v + upper * (n_lat - 1 - 2 * v)
+
+    def pick(v, values):
+        return sum(value * same(v, i) for i, value in enumerate(values))
+
+    targets = [pick(z, [TARGETS[i][k] for i in range(n_lat)]) for k in range(n_lat - 1)]
+    first = [pick(z, [FIRST[i][k] for i in range(n_lat)]) for k in range(n_lat)]
+    second = [pick(z, [SECOND[i][k] for i in range(n_lat)]) for k in range(n_lat)]
 
     def lay_peer(k):
         return {"lay": flip(l, k)}
 
     barrier = pltpu.get_barrier_semaphore()
     for k in range(n_lat - 1):
-        pl.semaphore_signal(
-            barrier, inc=1, device_id={"lat": farthest(k)}, device_id_type=MESH
-        )
+        pl.semaphore_signal(barrier, inc=1, device_id={"lat": targets[k]}, device_id_type=MESH)
     for k in reversed(range(1, n_lay)):
         pl.semaphore_signal(barrier, inc=1, device_id=lay_peer(k), device_id_type=MESH)
 
@@ -223,14 +227,9 @@
             whole += buf[k, flip(l, i)].astype(F32)
         return whole
 
-    first = [
-        z + k - (1 - lax.div(1, 1 + lax.div(z + k, n_lat))) * (z + 2 * k + 1 - n_lat)
-        for k in range(n_lat)
-    ]
-
     load_acts.wait()
     for k in range(n_lat - 1):
-        send(acts_all.at[z], acts_all.at[z], acts_s, acts_r.at[z], {"lat": farthest(k)})
+        send(acts_all.at[z], acts_all.at[z], acts_s, acts_r.at[z], {"lat": targets[k]})
     load_enc.wait()
 
     def encode(k):
@@ -247,12 +246,11 @@
         code = (0.25 * (jnp.maximum(x, 0.0) + jnp.log1p(e))).astype(BF16)
         rec = jnp.dot(code, wdec[...], preferred_element_type=F32).astype(BF16)
         rec_mine[b] = rec
-        owner = high - lax.div(b, half)
+        owner = pick(b, OWNER)
 
         @pl.when(owner != z)
         def _():
-            place = lax.rem(b, half)
-            send(rec_mine.at[b], rec_buf.at[place, z], rec_s, rec_r.at[place], {"lat": owner})
+            send(rec_mine.at[b], rec_buf.at[b, z], rec_s, rec_r.at[b], {"lat": owner})
 
         code_all[b] = code
         slope[b] = jnp.where(x >= 0.0, 1.0, e) / (1.0 + e)
@@ -268,29 +266,25 @@
     for k in range(n_lat):
         decode(k)
 
-    @pl.when((z == low) | (z == high))
-    def _():
-        for j in range(half):
-            b = half + j - same(z, high) * (2 * j + 1)
-            place = lax.rem(b, half)
-            wait(rec_buf.at[place, pl.ds(0, n_lat - 1)], rec_r.at[place])
-            err = bdec[...] - acts_all[b].astype(F32) + rec_mine[b].astype(F32)
-            for i in range(1, n_lat):
-                err += rec_buf[place, flip(z, i)].astype(F32)
-            err_all[b] = err.astype(BF16)
-            for k in range(n_lat - 1):
-                send(err_all.at[b], err_all.at[b], err_s, err_r.at[b], {"lat": farthest(k)})
+    for i, owned in enumerate(OWNED):
+        if owned:
+
+            @pl.when(z == i)
+            def _():
+                for b in owned:
+                    wait(rec_buf.at[b, pl.ds(0, n_lat - 1)], rec_r.at[b])
+                    err = bdec[...] - acts_all[b].astype(F32) + rec_mine[b].astype(F32)
+                    for j in SPREAD[i]:
+                        err += rec_buf[b, j].astype(F32)
+                    err_all[b] = err.astype(BF16)
+                    for j in SPREAD[i]:
+                        send(err_all.at[b], err_all.at[b], err_s, err_r.at[b], {"lat": j})
 
     code_t = code_all[...].reshape(rows, lat_dev).astype(F32).T.astype(BF16)
-    second = []
     for k in range(n_lat):
-        up = half + k if k < half else n_lat - 1 - k
-        down = half - 1 - k if k < half else k
-        b = up + same(z, high) * (down - up)
-        second.append(b)
-        owner = high - lax.div(b, half)
-
-        @pl.when(owner != z)
+        b = second[k]
+
+        @pl.when(pick(b, OWNER) != z)
         def _():
             wait(err_all.at[b], err_r.at[b])
 
@@ -306,15 +300,13 @@
     wait(acts_all.at[pl.ds(0, n_lat - 1)], acts_s)
     wait(pre_buf.at[:, pl.ds(1, n_lay - 1)], pre_s)
     wait(back_buf.at[:, pl.ds(1, n_lay - 1)], back_s)
-
-    @pl.when((z == low) | (z == high))
-    def _():
-        wait(rec_mine.at[pl.ds(0, half)], rec_s)
-        wait(rec_buf.at[:, pl.ds(0, n_lat - 1)], err_s)
-
-    @pl.when((z != low) & (z != high))
-    def _():
-        wait(rec_mine, rec_s)
+    for i, owned in enumerate(OWNED):
+
+        @pl.when(z == i)
+        def _():
+            wait(rec_mine.at[pl.ds(0, n_lat - len(owned))], rec_s)
+            if owned:
+                wait(rec_buf.at[pl.ds(0, len(owned)), pl.ds(0, n_lat - 1)], err_s)
 
 
 def finish(chunks, lat, acts_t, dec, lat_hbm, enc_hbm, dec_hbm, enc, sems):
@@ -347,7 +339,7 @@
         hbm = pl.BlockSpec(memory_space=pltpu.HBM)
         vmem = pl.BlockSpec(memory_space=pltpu.VMEM)
         dma = pltpu.SemaphoreType.DMA
-        line = n_lat in (2, 4) and n_lay & (n_lay - 1) == 0
+        line = n_lat == len(OWNER) and n_lay & (n_lay - 1) == 0
         groups = 4 if n_lat & (n_lat - 1) == 0 and n_lat % 4 == 0 else 1
         if line:
             groups = n_lat
@@ -373,14 +365,14 @@
                 lay_buf,
                 lay_buf,
                 rows_buf,
-                pltpu.VMEM((n_lat // 2, n_lat, row_dev, wide), BF16),
+                pltpu.VMEM((n_lat, n_lat, row_dev, wide), BF16),
                 rows_buf,
                 pltpu.VMEM((groups, part, lat_dev), BF16),
                 pltpu.VMEM((groups, part, lat_dev), F32),
                 dma((5,)),
                 dma, dma((n_lat,)),
                 dma, dma((groups,)),
-                dma, dma((n_lat // 2,)),
+                dma, dma((n_lat,)),
                 dma, dma((n_lat,)),
                 dma, dma((groups,)),
             ]

time: 26.1 us -> 25.9 us (level)
  no operation moved by 1% of the time
where the time goes in v2:
time: 25.9 us; the launch traced here: 25.8 us
  Pallas kernels  25.2 us (97%)
  between operations  0.64 us (2%)
    pallas_call x1, Pallas kernels, on_device(): pl.pallas_call(kernel, out_shape=out_shape, in_specs=in_specs, out_specs=...  23.8 us
    pallas_call x1, Pallas kernels, on_device(): pl.pallas_call(functools.partial(finish, chunks), out_shape=[jax.ShapeDty...  1.34 us

profile of v2, /device:TPU:0, one launch (start us, length us, event | category | flops | bytes accessed | tf_op | source)
XLA Modules:
  0.0 25.8 jit_solution(6253015415205706526)
XLA Ops:
  0.6 23.8 %shard_map.76 = (bf16[4,16,384]{2,1,0:T(8,128)(2,1)S(1)}, bf16[1280,64]{1,0:T(8,128)(2,1)S(1)}, bf16[384,1280]{1,0:T(8,128)(2,1)S(1)}) custom-call(bf16[16,1280]{1,0:T(8,128)(2,1)} %bitcast.8, bf16[1280,384]{1,0:T(8,128)(2,1)} %bitcast.6, bf16[384,1280]{1,0:T(8,128)(2,1)} %bitcast.7, f32[384]{0:T(512)} %benc_hbm.1, f32[1,1280]{1,0:T(1,128)} %bdec_hbm.1), custom_call_target="tpu_custom_call" | custom-call | flops 251658240 | bytes 1966080 | tf_op jit(solution)/shard_map/pallas_call | solution.py:401
  24.5 1.3 %shard_map.77 = (bf16[4,16,384]{2,1,0:T(8,128)(2,1)}, bf16[1280,384]{1,0:T(8,128)(2,1)}, bf16[384,1280]{1,0:T(8,128)(2,1)}) custom-call(bf16[4,16,384]{2,1,0:T(8,128)(2,1)S(1)} %get-tuple-element.9.lat, bf16[1280,64]{1,0:T(8,128)(2,1)S(1)} %get-tuple-element.10.acts_t, bf16[384,1280]{1,0:T(8,128)(2,1)S(1)} %get-tuple-element.11.dec), custom_call_target="tpu_custom_call" | custom-call | flops 62914560 | bytes 1966080 | tf_op jit(solution)/shard_map/pallas_call | solution.py:420

commit v3 on v2

--- a/solution.py
+++ b/solution.py
@@ -161,16 +161,17 @@
 
 OWNER = [2, 2, 1, 0]
 FIRST = [[0, 1, 2, 3], [1, 2, 3, 0], [2, 3, 1, 0], [3, 2, 1, 0]]
-SECOND = [[3, 2, 1, 0], [2, 3, 1, 0], [0, 1, 2, 3], [1, 0, 2, 3]]
+SECOND = [[3, 1, 2, 0], [2, 3, 1, 0], [0, 1, 2, 3], [1, 0, 2, 3]]
 OWNED = [[3], [2], [1, 0], []]
 TARGETS = [[3, 2, 1], [3, 2, 0], [0, 1, 3], [0, 1, 2]]
-SPREAD = [[1, 2, 3], [3, 2, 0], [0, 1, 3], []]
+SPREAD = [[0, 1, 2, 3], [0, 3, 2, 1], [0, 3, 2], []]
+LATER = [[], [], [(1, 1), (0, 1)], []]
 
 
 def line_step(
     n_lat, n_lay, acts_hbm, wenc_hbm, wdec_hbm, benc_hbm, bdec_hbm,
     lat_out, acts_t, dec_out,
-    acts_all, wenc, wdec, wdec_t, benc, bdec, pre_buf, back_buf, rec_mine, rec_buf, err_all,
+    acts_all, wenc, wdec, wdec_t, benc, bdec, pre_buf, back_buf, rec_mine, rec_buf, err_mine, err_all,
     code_all, slope,
     load, acts_s, acts_r, pre_s, pre_r, rec_s, rec_r, err_s, err_r, back_s, back_r,
 ):
@@ -244,13 +245,12 @@
         x = 4.0 * (total(pre_buf, k, pre_r) + benc[...].reshape(1, lat_dev))
         e = jnp.exp(-jnp.abs(x))
         code = (0.25 * (jnp.maximum(x, 0.0) + jnp.log1p(e))).astype(BF16)
-        rec = jnp.dot(code, wdec[...], preferred_element_type=F32).astype(BF16)
-        rec_mine[b] = rec
+        rec = jnp.dot(code, wdec[...], preferred_element_type=F32)
         owner = pick(b, OWNER)
-
-        @pl.when(owner != z)
-        def _():
-            send(rec_mine.at[b], rec_buf.at[b, z], rec_s, rec_r.at[b], {"lat": owner})
+        base = bdec[...] - acts_all[b].astype(F32)
+        rec_mine[b] = (rec + jnp.where(owner == z, base, 0.0)).astype(BF16)
+        peer = {"lat": owner, "lay": flip(l, 1)}
+        send(rec_mine.at[b], rec_buf.at[b, z], rec_s, rec_r.at[b], peer)
 
         code_all[b] = code
         slope[b] = jnp.where(x >= 0.0, 1.0, e) / (1.0 + e)
@@ -272,22 +272,22 @@
             @pl.when(z == i)
             def _():
                 for b in owned:
-                    wait(rec_buf.at[b, pl.ds(0, n_lat - 1)], rec_r.at[b])
-                    err = bdec[...] - acts_all[b].astype(F32) + rec_mine[b].astype(F32)
+                    wait(rec_buf.at[b], rec_r.at[b])
+                    err = rec_buf[b, 0].astype(F32)
+                    for j in range(1, n_lat):
+                        err += rec_buf[b, j].astype(F32)
+                    err_mine[b] = err.astype(BF16)
                     for j in SPREAD[i]:
-                        err += rec_buf[b, j].astype(F32)
-                    err_all[b] = err.astype(BF16)
-                    for j in SPREAD[i]:
-                        send(err_all.at[b], err_all.at[b], err_s, err_r.at[b], {"lat": j})
+                        peer = {"lat": j, "lay": flip(l, 1)}
+                        send(err_mine.at[b], err_all.at[b], err_s, err_r.at[b], peer)
+                for b, j in LATER[i]:
+                    peer = {"lat": j, "lay": flip(l, 1)}
+                    send(err_mine.at[b], err_all.at[b], err_s, err_r.at[b], peer)
 
     code_t = code_all[...].reshape(rows, lat_dev).astype(F32).T.astype(BF16)
     for k in range(n_lat):
         b = second[k]
-
-        @pl.when(pick(b, OWNER) != z)
-        def _():
-            wait(err_all.at[b], err_r.at[b])
-
+        wait(err_all.at[b], err_r.at[b])
         back = jnp.dot(err_all[b], wdec_t[...], preferred_element_type=F32)
         back_buf[k, 0] = back.astype(BF16)
         to_lay(back_buf, k, back_s, back_r)
@@ -300,13 +300,13 @@
     wait(acts_all.at[pl.ds(0, n_lat - 1)], acts_s)
     wait(pre_buf.at[:, pl.ds(1, n_lay - 1)], pre_s)
     wait(back_buf.at[:, pl.ds(1, n_lay - 1)], back_s)
+    wait(rec_mine, rec_s)
     for i, owned in enumerate(OWNED):
-
-        @pl.when(z == i)
-        def _():
-            wait(rec_mine.at[pl.ds(0, n_lat - len(owned))], rec_s)
-            if owned:
-                wait(rec_buf.at[pl.ds(0, len(owned)), pl.ds(0, n_lat - 1)], err_s)
+        if owned:
+
+            @pl.when(z == i)
+            def _():
+                wait(rec_buf.at[pl.ds(0, len(owned))], err_s)
 
 
 def finish(chunks, lat, acts_t, dec, lat_hbm, enc_hbm, dec_hbm, enc, sems):
@@ -339,7 +339,7 @@
         hbm = pl.BlockSpec(memory_space=pltpu.HBM)
         vmem = pl.BlockSpec(memory_space=pltpu.VMEM)
         dma = pltpu.SemaphoreType.DMA
-        line = n_lat == len(OWNER) and n_lay & (n_lay - 1) == 0
+        line = n_lat == len(OWNER) and n_lay & (n_lay - 1) == 0 and n_lay > 1
         groups = 4 if n_lat & (n_lat - 1) == 0 and n_lat % 4 == 0 else 1
         if line:
             groups = n_lat
@@ -366,6 +366,7 @@
                 lay_buf,
                 rows_buf,
                 pltpu.VMEM((n_lat, n_lat, row_dev, wide), BF16),
+                rows_buf,
                 rows_buf,
                 pltpu.VMEM((groups, part, lat_dev), BF16),
                 pltpu.VMEM((groups, part, lat_dev), F32),

time: 25.9 us -> 25.3 us (0.977)
  Pallas kernels: 25.2 us -> 24.5 us
    pallas_call x1, Pallas kernels: 23.8 us -> 23.2 us  [on_device(): pl.pallas_call(kernel, out_shape=out_shape, in_specs=in_specs, out_specs=...]
where the time goes in v3:
time: 25.3 us; the launch traced here: 25.2 us
  Pallas kernels  24.5 us (97%)
  between operations  0.64 us (3%)
    pallas_call x1, Pallas kernels, on_device(): pl.pallas_call(kernel, out_shape=out_shape, in_specs=in_specs, out_specs=...  23.2 us
    pallas_call x1, Pallas kernels, on_device(): pl.pallas_call(functools.partial(finish, chunks), out_shape=[jax.ShapeDty...  1.34 us

profile of v3, /device:TPU:0, one launch (start us, length us, event | category | flops | bytes accessed | tf_op | source)
XLA Modules:
  0.0 25.2 jit_solution(6898444503558612407)
XLA Ops:
  0.6 23.2 %shard_map.76 = (bf16[4,16,384]{2,1,0:T(8,128)(2,1)S(1)}, bf16[1280,64]{1,0:T(8,128)(2,1)S(1)}, bf16[384,1280]{1,0:T(8,128)(2,1)S(1)}) custom-call(bf16[16,1280]{1,0:T(8,128)(2,1)} %bitcast.8, bf16[1280,384]{1,0:T(8,128)(2,1)} %bitcast.6, bf16[384,1280]{1,0:T(8,128)(2,1)} %bitcast.7, f32[384]{0:T(512)} %benc_hbm.1, f32[1,1280]{1,0:T(1,128)} %bdec_hbm.1), custom_call_target="tpu_custom_call" | custom-call | flops 251658240 | bytes 1966080 | tf_op jit(solution)/shard_map/pallas_call | solution.py:402
  23.8 1.3 %shard_map.77 = (bf16[4,16,384]{2,1,0:T(8,128)(2,1)}, bf16[1280,384]{1,0:T(8,128)(2,1)}, bf16[384,1280]{1,0:T(8,128)(2,1)}) custom-call(bf16[4,16,384]{2,1,0:T(8,128)(2,1)S(1)} %get-tuple-element.9.lat, bf16[1280,64]{1,0:T(8,128)(2,1)S(1)} %get-tuple-element.10.acts_t, bf16[384,1280]{1,0:T(8,128)(2,1)S(1)} %get-tuple-element.11.dec), custom_call_target="tpu_custom_call" | custom-call | flops 62914560 | bytes 1966080 | tf_op jit(solution)/shard_map/pallas_call | solution.py:421

commit v4 on v3

--- a/solution.py
+++ b/solution.py
@@ -189,6 +189,7 @@
     def lay_peer(k):
         return {"lay": flip(l, k)}
 
+    odd = lax.rem(l, 2)
     barrier = pltpu.get_barrier_semaphore()
     for k in range(n_lat - 1):
         pl.semaphore_signal(barrier, inc=1, device_id={"lat": targets[k]}, device_id_type=MESH)
@@ -218,8 +219,11 @@
         pltpu.make_async_copy(view, view, sem).wait()
 
     def to_lay(buf, k, sent, received):
-        for j in sorted(range(1, n_lay), key=lambda j: (j < 2, j)):
-            send(buf.at[k, 0], buf.at[k, j], sent, received.at[k], lay_peer(j))
+        for j in (2, 3):
+            slot = j + odd * (5 - 2 * j)
+            peer = flip(l, j) + odd * (flip(l, 5 - j) - flip(l, j))
+            send(buf.at[k, 0], buf.at[k, slot], sent, received.at[k], {"lay": peer})
+        send(buf.at[k, 0], buf.at[k, 1], sent, received.at[k], lay_peer(1))
 
     def total(buf, k, received):
         wait(buf.at[k, pl.ds(1, n_lay - 1)], received.at[k])
@@ -251,7 +255,6 @@
         rec_mine[b] = (rec + jnp.where(owner == z, base, 0.0)).astype(BF16)
         peer = {"lat": owner, "lay": flip(l, 1)}
         send(rec_mine.at[b], rec_buf.at[b, z], rec_s, rec_r.at[b], peer)
-
         code_all[b] = code
         slope[b] = jnp.where(x >= 0.0, 1.0, e) / (1.0 + e)
 
@@ -339,7 +342,7 @@
         hbm = pl.BlockSpec(memory_space=pltpu.HBM)
         vmem = pl.BlockSpec(memory_space=pltpu.VMEM)
         dma = pltpu.SemaphoreType.DMA
-        line = n_lat == len(OWNER) and n_lay & (n_lay - 1) == 0 and n_lay > 1
+        line = n_lat == len(OWNER) and n_lay == 4
         groups = 4 if n_lat & (n_lat - 1) == 0 and n_lat % 4 == 0 else 1
         if line:
             groups = n_lat

time: 25.3 us -> 25.1 us (level)
  no operation moved by 1% of the time
where the time goes in v4:
time: 25.1 us; the launch traced here: 25 us
  Pallas kernels  24.3 us (97%)
  between operations  0.64 us (3%)
    pallas_call x1, Pallas kernels, on_device(): pl.pallas_call(kernel, out_shape=out_shape, in_specs=in_specs, out_specs=...  23 us
    pallas_call x1, Pallas kernels, on_device(): pl.pallas_call(functools.partial(finish, chunks), out_shape=[jax.ShapeDty...  1.34 us

profile of v4, /device:TPU:0, one launch (start us, length us, event | category | flops | bytes accessed | tf_op | source)
XLA Modules:
  0.0 25.0 jit_solution(13572340572243910584)
XLA Ops:
  0.6 23.0 %shard_map.76 = (bf16[4,16,384]{2,1,0:T(8,128)(2,1)S(1)}, bf16[1280,64]{1,0:T(8,128)(2,1)S(1)}, bf16[384,1280]{1,0:T(8,128)(2,1)S(1)}) custom-call(bf16[16,1280]{1,0:T(8,128)(2,1)} %bitcast.8, bf16[1280,384]{1,0:T(8,128)(2,1)} %bitcast.6, bf16[384,1280]{1,0:T(8,128)(2,1)} %bitcast.7, f32[384]{0:T(512)} %benc_hbm.1, f32[1,1280]{1,0:T(1,128)} %bdec_hbm.1), custom_call_target="tpu_custom_call" | custom-call | flops 251658240 | bytes 1966080 | tf_op jit(solution)/shard_map/pallas_call | solution.py:405
  23.6 1.3 %shard_map.77 = (bf16[4,16,384]{2,1,0:T(8,128)(2,1)}, bf16[1280,384]{1,0:T(8,128)(2,1)}, bf16[384,1280]{1,0:T(8,128)(2,1)}) custom-call(bf16[4,16,384]{2,1,0:T(8,128)(2,1)S(1)} %get-tuple-element.9.lat, bf16[1280,64]{1,0:T(8,128)(2,1)S(1)} %get-tuple-element.10.acts_t, bf16[384,1280]{1,0:T(8,128)(2,1)S(1)} %get-tuple-element.11.dec), custom_call_target="tpu_custom_call" | custom-call | flops 62914560 | bytes 1966080 | tf_op jit(solution)/shard_map/pallas_call | solution.py:424

commit v5 on v4

--- a/solution.py
+++ b/solution.py
@@ -253,8 +253,12 @@
         owner = pick(b, OWNER)
         base = bdec[...] - acts_all[b].astype(F32)
         rec_mine[b] = (rec + jnp.where(owner == z, base, 0.0)).astype(BF16)
-        peer = {"lat": owner, "lay": flip(l, 1)}
-        send(rec_mine.at[b], rec_buf.at[b, z], rec_s, rec_r.at[b], peer)
+
+        @pl.when((odd == 0) | (owner != z))
+        def _():
+            peer = {"lat": owner, "lay": l + 1 - odd}
+            send(rec_mine.at[b], rec_buf.at[odd, b, z], rec_s, rec_r.at[odd, b], peer)
+
         code_all[b] = code
         slope[b] = jnp.where(x >= 0.0, 1.0, e) / (1.0 + e)
 
@@ -272,25 +276,40 @@
     for i, owned in enumerate(OWNED):
         if owned:
 
-            @pl.when(z == i)
+            @pl.when((z == i) & (odd == 1))
             def _():
                 for b in owned:
-                    wait(rec_buf.at[b], rec_r.at[b])
-                    err = rec_buf[b, 0].astype(F32)
+                    wait(rec_buf.at[0, b], rec_r.at[0, b])
+                    err = rec_buf[0, b, 0].astype(F32)
                     for j in range(1, n_lat):
-                        err += rec_buf[b, j].astype(F32)
+                        err += rec_buf[0, b, j].astype(F32)
                     err_mine[b] = err.astype(BF16)
                     for j in SPREAD[i]:
                         peer = {"lat": j, "lay": flip(l, 1)}
-                        send(err_mine.at[b], err_all.at[b], err_s, err_r.at[b], peer)
+                        send(err_mine.at[b], err_all.at[b], err_s.at[0], err_r.at[b], peer)
+                    wait(rec_buf.at[1, b, pl.ds(0, n_lat - 1)], rec_r.at[1, b])
+                    err = rec_mine[b].astype(F32)
+                    for j in range(n_lat):
+                        if j != i:
+                            err += rec_buf[1, b, j].astype(F32)
+                    err_all[b] = err.astype(BF16)
+                    for j in SPREAD[i]:
+                        if j != i:
+                            peer = {"lat": j}
+                            send(err_all.at[b], err_all.at[b], err_s.at[1], err_r.at[b], peer)
                 for b, j in LATER[i]:
                     peer = {"lat": j, "lay": flip(l, 1)}
-                    send(err_mine.at[b], err_all.at[b], err_s, err_r.at[b], peer)
+                    send(err_mine.at[b], err_all.at[b], err_s.at[0], err_r.at[b], peer)
+                    send(err_all.at[b], err_all.at[b], err_s.at[1], err_r.at[b], {"lat": j})
 
     code_t = code_all[...].reshape(rows, lat_dev).astype(F32).T.astype(BF16)
     for k in range(n_lat):
         b = second[k]
-        wait(err_all.at[b], err_r.at[b])
+
+        @pl.when((odd == 0) | (pick(b, OWNER) != z))
+        def _():
+            wait(err_all.at[b], err_r.at[b])
+
         back = jnp.dot(err_all[b], wdec_t[...], preferred_element_type=F32)
         back_buf[k, 0] = back.astype(BF16)
         to_lay(back_buf, k, back_s, back_r)
@@ -303,13 +322,18 @@
     wait(acts_all.at[pl.ds(0, n_lat - 1)], acts_s)
     wait(pre_buf.at[:, pl.ds(1, n_lay - 1)], pre_s)
     wait(back_buf.at[:, pl.ds(1, n_lay - 1)], back_s)
-    wait(rec_mine, rec_s)
+    @pl.when(odd == 0)
+    def _():
+        wait(rec_mine, rec_s)
+
     for i, owned in enumerate(OWNED):
-        if owned:
-
-            @pl.when(z == i)
-            def _():
-                wait(rec_buf.at[pl.ds(0, len(owned))], err_s)
+
+        @pl.when((z == i) & (odd == 1))
+        def _():
+            wait(rec_mine.at[pl.ds(0, n_lat - len(owned))], rec_s)
+            if owned:
+                wait(rec_buf.at[0, pl.ds(0, len(owned))], err_s.at[0])
+                wait(rec_buf.at[0, pl.ds(0, len(owned)), pl.ds(0, n_lat - 1)], err_s.at[1])
 
 
 def finish(chunks, lat, acts_t, dec, lat_hbm, enc_hbm, dec_hbm, enc, sems):
@@ -368,7 +392,7 @@
                 lay_buf,
                 lay_buf,
                 rows_buf,
-                pltpu.VMEM((n_lat, n_lat, row_dev, wide), BF16),
+                pltpu.VMEM((2, n_lat, n_lat, row_dev, wide), BF16),
                 rows_buf,
                 rows_buf,
                 pltpu.VMEM((groups, part, lat_dev), BF16),
@@ -376,8 +400,8 @@
                 dma((5,)),
                 dma, dma((n_lat,)),
                 dma, dma((groups,)),
-                dma, dma((n_lat,)),
-                dma, dma((n_lat,)),
+                dma, dma((2, n_lat)),
+                dma((2,)), dma((n_lat,)),
                 dma, dma((groups,)),
             ]
         else:

time: 25.1 us -> 25 us (level)
  no operation moved by 1% of the time
where the time goes in v5:
time: 25 us; the launch traced here: 24.9 us
  Pallas kernels  24.2 us (97%)
  between operations  0.64 us (3%)
    pallas_call x1, Pallas kernels, on_device(): pl.pallas_call(kernel, out_shape=out_shape, in_specs=in_specs, out_specs=...  22.9 us
    pallas_call x1, Pallas kernels, on_device(): pl.pallas_call(functools.partial(finish, chunks), out_shape=[jax.ShapeDty...  1.34 us

profile of v5, /device:TPU:0, one launch (start us, length us, event | category | flops | bytes accessed | tf_op | source)
XLA Modules:
  0.0 24.9 jit_solution(13451745029632373361)
XLA Ops:
  0.6 22.9 %shard_map.76 = (bf16[4,16,384]{2,1,0:T(8,128)(2,1)S(1)}, bf16[1280,64]{1,0:T(8,128)(2,1)S(1)}, bf16[384,1280]{1,0:T(8,128)(2,1)S(1)}) custom-call(bf16[16,1280]{1,0:T(8,128)(2,1)} %bitcast.8, bf16[1280,384]{1,0:T(8,128)(2,1)} %bitcast.6, bf16[384,1280]{1,0:T(8,128)(2,1)} %bitcast.7, f32[384]{0:T(512)} %benc_hbm.1, f32[1,1280]{1,0:T(1,128)} %bdec_hbm.1), custom_call_target="tpu_custom_call" | custom-call | flops 251658240 | bytes 1966080 | tf_op jit(solution)/shard_map/pallas_call | solution.py:429
  23.5 1.3 %shard_map.77 = (bf16[4,16,384]{2,1,0:T(8,128)(2,1)}, bf16[1280,384]{1,0:T(8,128)(2,1)}, bf16[384,1280]{1,0:T(8,128)(2,1)}) custom-call(bf16[4,16,384]{2,1,0:T(8,128)(2,1)S(1)} %get-tuple-element.9.lat, bf16[1280,64]{1,0:T(8,128)(2,1)S(1)} %get-tuple-element.10.acts_t, bf16[384,1280]{1,0:T(8,128)(2,1)S(1)} %get-tuple-element.11.dec), custom_call_target="tpu_custom_call" | custom-call | flops 62914560 | bytes 1966080 | tf_op jit(solution)/shard_map/pallas_call | solution.py:448
